TPU v7x, 512 devices: a 4x2x32 block of a 4x8x32 slice. The times are simulated.
512 devices in a mesh: groups: 2 (over y), aa: 32 (over z), ba: 4 (over x), col: 2 (over core).
Axes of the slice: x: 4, y: 2, z: 32, core: 2. Of those that a mesh axis runs over, the one named last changes fastest.
The devices are a block of a 4x8x32 slice.
Arguments:
- hidden: bfloat16 [256, 128, 8192], P(('groups', 'aa'), None, ('ba', 'col')), parts along dimension 0, may hold values from -6 to 6
- key_value_weight: bfloat16 [2048, 8192], P('aa', ('ba', 'col')), may hold values from -0.125 to 0.125
- adapter_down_weight: bfloat16 [256, 32, 8192], P(('groups', 'aa'), None, ('ba', 'col')), parts along dimension 0, may hold values from -0.0625 to 0.0625
- adapter_up_weight: bfloat16 [256, 16, 2048], P(('groups', 'aa'), None, ('ba', 'col')), parts along dimension 0, may hold values from -1.5 to 1.5
- prompt_block_count: int32 [128], P('groups'), parts along dimension 0, may hold values from 1 to 3, 128 in all
- request_adapter: int32 [128], P('groups'), parts along dimension 0, may hold values from 0 to 127
- adapter_bank_row: int32 [256], P('groups'), parts along dimension 0, may hold values from 0 to 127, each once
Outputs:
- kv_states: bfloat16 [256, 128, 2048], P(('groups', 'aa'), None, ('ba', 'col')), parts along dimension 0
There are 2 independent parts, one for each index of `groups`. A program takes and returns all parts, laid end to end along the dimension named above; an argument that names none is the same for every part. Nothing has to cross between parts.
Inputs may be any that keep to these rules, and one draw needn't show every extreme that they name: prompt_block_count sum to 128; some request has exactly 3 blocks. `adapter_bank_row`: each bank row holds one adapter; bank row s lies on index s // 4 of aa.
All inputs are finite; a program needn't handle non-finite values.
Results may differ from a plain program's by a relative error of at most 0.001.
Values may be sent and summed in bfloat16 or wider, within the bound.
No kernel may reach another device: no remote copies, remote signals or barrier semaphores. Data moves between devices by JAX's collectives and lax.ppermute only.
A program may use at most 128 MiB of HBM per device.

v0:
```python
import math
import jax
import jax.numpy as jnp
from jax import lax
from jax.sharding import PartitionSpec as P


def side_by_side(arrays, axis, dim, along):
    widths = [math.prod(a.shape[along:]) for a in arrays]
    both = jnp.concatenate(
        [a.reshape(*a.shape[:along], w) for a, w in zip(arrays, widths)], axis=along
    )
    out = lax.all_gather(both, axis, axis=dim, tiled=True)
    parts = jnp.split(out, [sum(widths[:k]) for k in range(1, len(widths))], axis=along)
    return tuple((b.reshape(*out.shape[:along], *a.shape[along:]) for a, b in zip(arrays, parts)))


def from_everyone(x, axis):
    copies = jnp.broadcast_to(x, (lax.axis_size(axis), *x.shape))
    return lax.all_to_all(copies, axis, split_axis=0, concat_axis=0, tiled=True)


def of_everyone(x, axis):
    return from_everyone(x, axis).sum(axis=0)


def block_slots(prompt_block_count, request_adapter, adapter_bank_row, block_total):
    block_ids = jnp.arange(block_total, dtype=jnp.int32)
    block_ends = jnp.cumsum(prompt_block_count)
    request_of = jnp.sum((block_ends[None, :] <= block_ids[:, None]).astype(jnp.int32), axis=1)
    request_ids = jnp.arange(prompt_block_count.shape[0], dtype=jnp.int32)
    adapter_of = jnp.sum(
        jnp.where(request_of[:, None] == request_ids[None, :], request_adapter[None, :], 0), axis=1
    )
    adapter_rows = jnp.arange(adapter_bank_row.shape[0], dtype=jnp.int32)
    return jnp.sum(
        jnp.where(adapter_of[:, None] == adapter_rows[None, :], adapter_bank_row[None, :], 0),
        axis=1,
    )


def body(
    hidden,
    key_value_weight,
    adapter_down_weight,
    adapter_up_weight,
    prompt_block_count,
    request_adapter,
    adapter_bank_row,
):
    owners = lax.axis_size("aa")
    owner_index = lax.axis_index("aa")
    shard_count = lax.axis_size(("ba", "col"))
    local_blocks, block_len, feat_width = hidden.shape
    request_grouped, paired_rank, unused_item = adapter_down_weight.shape
    rank_half = paired_rank // 2
    column_span = adapter_up_weight.shape[2]
    bank_row_lookup = block_slots(
        prompt_block_count, request_adapter, adapter_bank_row, local_blocks * owners
    )
    my_slots = lax.dynamic_slice_in_dim(bank_row_lookup, owner_index * local_blocks, local_blocks)
    token_rows = hidden.reshape(local_blocks * block_len, feat_width)
    partial_sums = lax.dot_general(
        token_rows,
        lax.all_gather(key_value_weight, "aa", axis=0, tiled=True),
        (((1,), (1,)), ((), ())),
        preferred_element_type=jnp.float32,
    )
    down_weight_slice, up_weight_slice = side_by_side(
        (adapter_down_weight, adapter_up_weight), "aa", 0, 1
    )
    bank_rows = jnp.arange(down_weight_slice.shape[0], dtype=jnp.int32)
    onehot = (my_slots[:, None] == bank_rows[None, :]).astype(jnp.bfloat16)
    down_add = jnp.einsum(
        "cn,nrf->crf", onehot, down_weight_slice, preferred_element_type=jnp.float32
    )
    up_weight_extra = jnp.einsum(
        "cn,nrj->crj", onehot, up_weight_slice, preferred_element_type=jnp.float32
    )
    down_sel = down_add
    down_sel = down_sel.astype(jnp.bfloat16)
    base_output = lax.psum_scatter(partial_sums, ("ba", "col"), scatter_dimension=1, tiled=True)
    low_part = jnp.einsum("ctf,crf->ctr", hidden, down_sel, preferred_element_type=jnp.float32)
    low_rank = of_everyone(low_part, ("ba", "col"))
    first_col = lax.axis_index(("ba", "col")) * column_span
    active_rank = jnp.where(
        first_col < column_span * shard_count // 2,
        low_rank[:, :, :rank_half],
        low_rank[:, :, rank_half:],
    )
    adapter_output = jnp.einsum(
        "qvy,qyz->qvz", active_rank, up_weight_extra, precision=lax.Precision.HIGHEST
    )
    base_output = base_output.reshape(local_blocks, block_len, column_span)
    return (base_output + adapter_output).astype(jnp.bfloat16)


def solution(mesh):
    placed = (
        P(("groups", "aa"), None, ("ba", "col")),
        P("aa", ("ba", "col")),
        P(("groups", "aa"), None, ("ba", "col")),
        P(("groups", "aa"), None, ("ba", "col")),
        P("groups"),
        P("groups"),
        P("groups"),
    )
    return jax.shard_map(
        body,
        mesh=mesh,
        in_specs=placed,
        out_specs=P(("groups", "aa"), None, ("ba", "col")),
        check_vma=False,
    )
```

profile of v0, /device:TPU:33, one launch (start us, length us, event | category | flops | bytes accessed | tf_op | source)
XLA Modules:
  0.0 386.0 jit_solution(8711361571595567866)
XLA Ops:
  6.5 0.0 copy-start
  6.6 0.0 all-gather.4.cloned.1.call-start
  6.6 0.7 all-gather.4.cloned.1.call-update
  7.3 0.1 all-gather.6.cloned.1.call-start
  7.4 0.8 copy.38
  8.2 1.2 copy.37
  9.3 0.9 maximum_bitcast_fusion
  10.2 0.1 all-gather.6.cloned.1.call-update
  10.2 0.1 reduce-scatter.2.cloned.1.call-start
  10.3 145.4 %all-gather.4.cloned.1.call-done = bf16[2048,1024]{1,0:T(8,128)(2,1)} async-done(((bf16[64,1024]{1,0:T(8,128)(2,1)}), bf16[2048,1024]{1,0:T(8,128)(2,1)}) %all-gather.4.cloned.1.call-update) | async-done | bytes 4194320 | tf_op jit(solution)/shard_map/all_gather | solution.py:65
  155.7 0.0 copy-done
  155.8 0.0 copy-start.1
  155.8 0.0 copy-start.2
  155.8 0.0 copy-start.3
  155.8 6.7 %fusion.11 = f32[512,2048]{1,0:T(8,128)} fusion(bf16[512,1024]{1,0:T(8,128)(2,1)S(1)} %bitcast.22, bf16[2048,1024]{1,0:T(8,128)(2,1)} %all-gather.4.cloned.1.call-done), kind=kOutput, calls=%fused_computation.21 | convolution fusion | flops 2147483648 | bytes 9437184 | tf_op jit(solution)/shard_map/dot_general | solution.py:63
  162.4 0.1 reduce-scatter.2.cloned.1.call-update
  162.5 0.0 copy-done.1
  162.5 0.1 copy.28
  162.6 0.1 reduce-window.8
  162.7 0.1 reduce
  162.8 0.1 convert_reduce_fusion
  162.9 0.0 copy-done.2
  162.9 0.1 select_reduce_fusion.1
  163.0 0.0 copy-done.3
  163.0 0.2 select_reduce_fusion
  163.2 0.1 dynamic_slice.3
  163.3 140.5 %all-gather.6.cloned.1.call-done = bf16[32,4,36864]{2,1,0:T(4,128)(2,1)} async-done(((bf16[1,4,36864]{2,1,0:T(4,128)(2,1)}), bf16[32,4,36864]{2,1,0:T(4,128)(2,1)}) %all-gather.6.cloned.1.call-update) | async-done | bytes 9437200 | tf_op jit(solution)/shard_map/all_gather | solution.py:13
  303.8 13.3 %reshape.56 = bf16[128,36864]{1,0:T(8,128)(2,1)} reshape(bf16[32,4,36864]{2,1,0:T(4,128)(2,1)} %all-gather.6.cloned.1.call-done) | data formatting | bytes 18874368
  317.1 7.4 %split.8 = bf16[128,32768]{1,0:T(8,128)(2,1)} slice(bf16[128,36864]{1,0:T(8,128)(2,1)} %reshape.56), slice={[0:128], [0:32768]} | slice | bytes 16777216 | tf_op jit(solution)/shard_map/split | solution.py:14
  324.5 12.0 %copy.29 = bf16[128,32768]{0,1:T(8,128)(2,1)} copy(bf16[128,32768]{1,0:T(8,128)(2,1)} %split.8) | data formatting | bytes 16777216 | tf_op jit(solution)/shard_map/split | solution.py:14
  336.5 0.0 slice-start
  336.5 5.8 %convolution_convert_fusion = bf16[4,32,1024]{2,0,1:T(4,128)(2,1)S(1)} fusion(bf16[128,32,1024]{0,2,1:T(8,128)(2,1)} %bitcast.23, s32[4]{0:T(128)S(1)} %dynamic_slice.3), kind=kOutput, calls=%fused_computation.2 | convolution fusion | flops 33686016 | bytes 8650768 | tf_op jit(solution)/shard_map/cn,nrf->crf/dot_general | solution.py:74
  342.3 0.5 convolution_bitcast_fusion
  342.7 0.9 broadcast_in_dim.41
  343.6 22.9 %all-to-all-start = ((f32[8,4,128,32]{2,3,1,0:T(8,128)}), f32[8,4,128,32]{2,3,1,0:T(8,128)}, u32[]{:S(2)}, u32[]{:S(2)}) async-start(f32[8,4,128,32]{2,3,1,0:T(8,128)} %broadcast_in_dim.41), calls=%async_computation.1 | async-start | bytes 1048576 | tf_op jit(solution)/shard_map/all_to_all | solution.py:20
  366.5 0.0 slice-done
  366.5 0.7 copy.32
  367.2 0.4 fusion.6
  367.6 8.4 %all-to-all-done = f32[8,4,128,32]{2,3,1,0:T(8,128)} async-done(((f32[8,4,128,32]{2,3,1,0:T(8,128)}), f32[8,4,128,32]{2,3,1,0:T(8,128)}, u32[]{:S(2)}, u32[]{:S(2)}) %all-to-all-start) | async-done | bytes 524320 | tf_op jit(solution)/shard_map/all_to_all | solution.py:20
  376.0 1.1 reduce_sum.39
  377.1 0.0 reduce-scatter.2.cloned.1.call-done
  377.1 2.4 fusion
Async XLA Ops:
  6.5 149.2 %copy-start = (bf16[4,128,1024]{2,1,0:T(8,128)(2,1)S(1)}, bf16[4,128,1024]{2,1,0:T(8,128)(2,1)}, u32[]{:S(2)}) copy-start(bf16[4,128,1024]{2,1,0:T(8,128)(2,1)} %param.7) | copy-start | bytes 3145732
  6.6 149.2 %all-gather.4.cloned.1.call-start = ((), (), s32[]{:S(2)}) async-start(), calls=%async_computation.2 | async-start | bytes 4325376 | tf_op jit(solution)/shard_map/all_gather | solution.py:65
  7.3 296.5 %all-gather.6.cloned.1.call-start = ((), (), s32[]{:S(2)}) async-start(), calls=%async_computation.4 | async-start | bytes 9732096 | tf_op jit(solution)/shard_map/all_gather | solution.py:13
  10.2 366.8 %reduce-scatter.2.cloned.1.call-start = ((), (), s32[]{:S(2)}) async-start(), calls=%async_computation.3 | async-start | bytes 4718592 | tf_op jit(solution)/shard_map/reduce_scatter | solution.py:82
  155.8 6.7 %copy-start.1 = (s32[64]{0:T(128)S(1)}, s32[64]{0:T(128)}, u32[]{:S(2)}) copy-start(s32[64]{0:T(128)} %param.11) | copy-start | bytes 772
  155.8 7.2 %copy-start.2 = (s32[64]{0:T(128)S(1)}, s32[64]{0:T(128)}, u32[]{:S(2)}) copy-start(s32[64]{0:T(128)} %param.12) | copy-start | bytes 772
  155.8 7.3 %copy-start.3 = (s32[128]{0:T(128)S(1)}, s32[128]{0:T(128)}, u32[]{:S(2)}) copy-start(s32[128]{0:T(128)} %param.13) | copy-start | bytes 1540
  336.5 30.0 %slice-start = ((bf16[128,36864]{1,0:T(8,128)(2,1)}), bf16[128,4096]{1,0:T(8,128)(2,1)S(1)}, s32[]{:S(2)}) async-start(bf16[128,36864]{1,0:T(8,128)(2,1)} %reshape.56), calls=%async_computation.5 | async-start | bytes 2097152 | tf_op jit(solution)/shard_map/split | solution.py:14
  343.6 32.4 %all-to-all-start = ((f32[8,4,128,32]{2,3,1,0:T(8,128)}), f32[8,4,128,32]{2,3,1,0:T(8,128)}, u32[]{:S(2)}, u32[]{:S(2)}) async-start(f32[8,4,128,32]{2,3,1,0:T(8,128)} %broadcast_in_dim.41), calls=%async_computation.1 | async-start | bytes 1048576 | tf_op jit(solution)/shard_map/all_to_all | solution.py:20
Sparse Core Ops, SparseCore 0:
  9.4 146.2 all-gather.3
  157.8 145.9 all-gather.5
  306.7 62.0 reduce-scatter.1
where the time goes:
time: 387 us; the launch traced here: 386 us
  waiting for transfers between devices  295 us (76%)
  local copies, waits for them, and re-layouts  36.3 us (9%)
  starting transfers between devices  23 us (6%)
  matrix products  15.7 us (4%)
  between operations  13.2 us (3%)
    all_gather x1, waiting for transfers between devices, body(): lax.all_gather(key_value_weight, 'aa', axis=0, tiled=True)  145 us
    all_gather x1, waiting for transfers between devices, side_by_side(): out = lax.all_gather(both, axis, axis=dim, tiled=True)  141 us
    all_to_all x1, starting transfers between devices, from_everyone(): return lax.all_to_all(copies, axis, split_axis=0, concat_axis=0, tiled=True)  22.9 us
    split x5, local copies, waits for them, and re-layouts, side_by_side(): jnp.split(out, [sum(widths[:k]) for k in range(1, len(widths))], axis=along)  20.1 us
    unnamed x11, local copies, waits for them, and re-layouts  15.2 us
    all_to_all x1, waiting for transfers between devices, from_everyone(): return lax.all_to_all(copies, axis, split_axis=0, concat_axis=0, tiled=True)  8.39 us
  transfers between devices with their start and end apart: 4, of which 3 were waited for; matrix products, arithmetic and copies ran while one was open for 14% of the time, Pallas kernels for 0%

commit v1 on v0

--- a/solution.py
+++ b/solution.py
@@ -3,6 +3,14 @@
 import jax.numpy as jnp
 from jax import lax
 from jax.sharding import PartitionSpec as P
+
+
+def gather_from_all(shard, axis, dim):
+    size = lax.axis_size(axis)
+    repeats = [size if d == dim else 1 for d in range(shard.ndim)]
+    return lax.all_to_all(
+        jnp.tile(shard, repeats), axis, split_axis=dim, concat_axis=dim, tiled=True
+    )
 
 
 def side_by_side(arrays, axis, dim, along):
@@ -62,7 +70,7 @@
     token_rows = hidden.reshape(local_blocks * block_len, feat_width)
     partial_sums = lax.dot_general(
         token_rows,
-        lax.all_gather(key_value_weight, "aa", axis=0, tiled=True),
+        gather_from_all(key_value_weight, "aa", 0),
         (((1,), (1,)), ((), ())),
         preferred_element_type=jnp.float32,
     )

time: 387 us -> 602 us (1.56)
  waiting for transfers between devices: 295 us -> 468 us
  starting transfers between devices: 23 us -> 61.4 us
    all_to_all x0 -> x1, waiting for transfers between devices: none -> 419 us  [gather_from_all(): lax.all_to_all(jnp.tile(shard, repeats), axis, split_axis=dim, concat_axi...]
    all_gather x1 -> x0, waiting for transfers between devices: 145 us -> none  [body(): lax.all_gather(key_value_weight, 'aa', axis=0, tiled=True)]
    all_gather x1, waiting for transfers between devices: 141 us -> 40.6 us  [side_by_side(): out = lax.all_gather(both, axis, axis=dim, tiled=True)]
    all_to_all x0 -> x1, starting transfers between devices: none -> 46.3 us  [gather_from_all(): lax.all_to_all(jnp.tile(shard, repeats), axis, split_axis=dim, concat_axi...]
    all_to_all x1, starting transfers between devices: 22.9 us -> 14.9 us  [from_everyone(): return lax.all_to_all(copies, axis, split_axis=0, concat_axis=0, tiled=True)]
    unnamed x11 -> x15, local copies, waits for them, and re-layouts: 15.2 us -> 13.5 us
  transfers between devices with their start and end apart: 4 -> 4, of which waited for: 3 -> 3; matrix products, arithmetic and copies ran while one was open for 14% -> 8% of each run, Pallas kernels for 0% -> 0%
where the time goes in v1:
time: 602 us; the launch traced here: 601 us
  waiting for transfers between devices  468 us (78%)
  starting transfers between devices  61.4 us (10%)
  local copies, waits for them, and re-layouts  38.1 us (6%)
  matrix products  15.7 us (3%)
  between operations  15 us (2%)
    all_to_all x1, waiting for transfers between devices, gather_from_all(): lax.all_to_all(jnp.tile(shard, repeats), axis, split_axis=dim, concat_axi...  419 us
    all_to_all x1, starting transfers between devices, gather_from_all(): lax.all_to_all(jnp.tile(shard, repeats), axis, split_axis=dim, concat_axi...  46.3 us
    all_gather x1, waiting for transfers between devices, side_by_side(): out = lax.all_gather(both, axis, axis=dim, tiled=True)  40.6 us
    split x5, local copies, waits for them, and re-layouts, side_by_side(): jnp.split(out, [sum(widths[:k]) for k in range(1, len(widths))], axis=along)  20.1 us
    all_to_all x1, starting transfers between devices, from_everyone(): return lax.all_to_all(copies, axis, split_axis=0, concat_axis=0, tiled=True)  14.9 us
    unnamed x15, local copies, waits for them, and re-layouts  13.5 us
  transfers between devices with their start and end apart: 4, of which 3 were waited for; matrix products, arithmetic and copies ran while one was open for 8% of the time, Pallas kernels for 0%

profile of v1, /device:TPU:33, one launch (start us, length us, event | category | flops | bytes accessed | tf_op | source)
XLA Modules:
  0.0 601.0 jit_solution(4712072963880281722)
XLA Ops:
  7.4 0.0 copy-start
  7.4 0.0 copy-start.2
  7.4 0.0 copy-start.1
  7.4 3.5 tile.2
  10.9 46.3 %all-to-all-start = ((bf16[32,64,1024]{2,1,0:T(8,128)(2,1)}), bf16[32,64,1024]{2,1,0:T(8,128)(2,1)}, u32[]{:S(2)}, u32[]{:S(2)}) async-start(bf16[32,64,1024]{2,1,0:T(8,128)(2,1)} %tile.2), calls=%async_computation | async-start | bytes 8388608 | tf_op jit(solution)/shard_map/all_to_all | solution.py:11
  57.2 0.1 all-gather.3.cloned.1.call-start
  57.3 0.0 copy-done.2
  57.3 0.0 copy-done.1
  57.3 0.2 copy.37
  57.5 0.9 maximum_bitcast_fusion
  58.4 0.1 all-gather.3.cloned.1.call-update
  58.5 0.1 reduce-scatter.2.cloned.1.call-start
  58.5 419.1 %all-to-all-done = bf16[32,64,1024]{2,1,0:T(8,128)(2,1)} async-done(((bf16[32,64,1024]{2,1,0:T(8,128)(2,1)}), bf16[32,64,1024]{2,1,0:T(8,128)(2,1)}, u32[]{:S(2)}, u32[]{:S(2)}) %all-to-all-start) | async-done | bytes 4194336 | tf_op jit(solution)/shard_map/all_to_all | solution.py:11
  477.6 0.0 copy-done
  477.6 0.0 copy-start.3
  477.6 0.0 copy-start.4
  477.6 0.0 copy-start.5
  477.6 6.7 %fusion.11 = f32[512,2048]{1,0:T(8,128)} fusion(bf16[512,1024]{1,0:T(8,128)(2,1)S(1)} %bitcast.23, bf16[2048,1024]{1,0:T(8,128)(2,1)} %bitcast.1), kind=kOutput, calls=%fused_computation.21 | convolution fusion | flops 2147483648 | bytes 9437184 | tf_op jit(solution)/shard_map/dot_general | solution.py:71
  484.3 0.1 reduce-scatter.2.cloned.1.call-update
  484.4 0.0 copy-done.3
  484.4 0.1 copy.28
  484.5 0.1 reduce-window.8
  484.6 0.1 reduce
  484.7 0.1 convert_reduce_fusion
  484.8 0.0 copy-done.4
  484.8 0.1 select_reduce_fusion.1
  484.9 0.0 copy-done.5
  484.9 0.2 select_reduce_fusion
  485.1 0.1 dynamic_slice.3
  485.2 40.6 %all-gather.3.cloned.1.call-done = bf16[32,4,36864]{2,1,0:T(4,128)(2,1)} async-done(((bf16[1,4,36864]{2,1,0:T(4,128)(2,1)}), bf16[32,4,36864]{2,1,0:T(4,128)(2,1)}) %all-gather.3.cloned.1.call-update) | async-done | bytes 9437200 | tf_op jit(solution)/shard_map/all_gather | solution.py:21
  525.7 13.3 %reshape.63 = bf16[128,36864]{1,0:T(8,128)(2,1)} reshape(bf16[32,4,36864]{2,1,0:T(4,128)(2,1)} %all-gather.3.cloned.1.call-done) | data formatting | bytes 18874368
  539.0 7.4 %split.8 = bf16[128,32768]{1,0:T(8,128)(2,1)} slice(bf16[128,36864]{1,0:T(8,128)(2,1)} %reshape.63), slice={[0:128], [0:32768]} | slice | bytes 16777216 | tf_op jit(solution)/shard_map/split | solution.py:22
  546.5 12.0 %copy.29 = bf16[128,32768]{0,1:T(8,128)(2,1)} copy(bf16[128,32768]{1,0:T(8,128)(2,1)} %split.8) | data formatting | bytes 16777216 | tf_op jit(solution)/shard_map/split | solution.py:22
  558.4 0.0 slice-start
  558.4 5.8 convolution_convert_fusion
  564.2 0.5 convolution_bitcast_fusion
  564.7 0.9 broadcast_in_dim.41
  565.6 14.9 %all-to-all-start.1 = ((f32[8,4,128,32]{2,3,1,0:T(8,128)}), f32[8,4,128,32]{2,3,1,0:T(8,128)}, u32[]{:S(2)}, u32[]{:S(2)}) async-start(f32[8,4,128,32]{2,3,1,0:T(8,128)} %broadcast_in_dim.41), calls=%async_computation.2 | async-start | bytes 1048576 | tf_op jit(solution)/shard_map/all_to_all | solution.py:28
  580.5 0.0 slice-done
  580.5 0.7 copy.32
  581.1 0.4 fusion.6
  581.5 8.5 %all-to-all-done.1 = f32[8,4,128,32]{2,3,1,0:T(8,128)} async-done(((f32[8,4,128,32]{2,3,1,0:T(8,128)}), f32[8,4,128,32]{2,3,1,0:T(8,128)}, u32[]{:S(2)}, u32[]{:S(2)}) %all-to-all-start.1) | async-done | bytes 524320 | tf_op jit(solution)/shard_map/all_to_all | solution.py:28
  590.0 1.1 reduce_sum.39
  591.1 0.0 reduce-scatter.2.cloned.1.call-done
  591.1 2.4 fusion
  (1 shorter events, 0.0 us)
Async XLA Ops:
  7.4 470.2 %copy-start = (bf16[4,128,1024]{2,1,0:T(8,128)(2,1)S(1)}, bf16[4,128,1024]{2,1,0:T(8,128)(2,1)}, u32[]{:S(2)}) copy-start(bf16[4,128,1024]{2,1,0:T(8,128)(2,1)} %param.7) | copy-start | bytes 3145732
  7.4 49.9 %copy-start.2 = (bf16[4,16,256]{2,1,0:T(8,128)(2,1)S(1)}, bf16[4,16,256]{2,1,0:T(8,128)(2,1)}, u32[]{:S(2)}) copy-start(bf16[4,16,256]{2,1,0:T(8,128)(2,1)} %param.10) | copy-start | bytes 98308
  7.4 49.9 %copy-start.1 = (bf16[4,32,1024]{2,1,0:T(8,128)(2,1)S(1)}, bf16[4,32,1024]{2,1,0:T(8,128)(2,1)}, u32[]{:S(2)}) copy-start(bf16[4,32,1024]{2,1,0:T(8,128)(2,1)} %param.9) | copy-start | bytes 786436
  10.9 466.7 %all-to-all-start = ((bf16[32,64,1024]{2,1,0:T(8,128)(2,1)}), bf16[32,64,1024]{2,1,0:T(8,128)(2,1)}, u32[]{:S(2)}, u32[]{:S(2)}) async-start(bf16[32,64,1024]{2,1,0:T(8,128)(2,1)} %tile.2), calls=%async_computation | async-start | bytes 8388608 | tf_op jit(solution)/shard_map/all_to_all | solution.py:11
  57.2 468.5 %all-gather.3.cloned.1.call-start = ((), (), s32[]{:S(2)}) async-start(), calls=%async_computation.4 | async-start | bytes 9732096 | tf_op jit(solution)/shard_map/all_gather | solution.py:21
  58.5 532.7 %reduce-scatter.2.cloned.1.call-start = ((), (), s32[]{:S(2)}) async-start(), calls=%async_computation.3 | async-start | bytes 4718592 | tf_op jit(solution)/shard_map/reduce_scatter | solution.py:90
  477.6 6.8 %copy-start.3 = (s32[64]{0:T(128)S(1)}, s32[64]{0:T(128)}, u32[]{:S(2)}) copy-start(s32[64]{0:T(128)} %param.11) | copy-start | bytes 772
  477.6 7.2 %copy-start.4 = (s32[64]{0:T(128)S(1)}, s32[64]{0:T(128)}, u32[]{:S(2)}) copy-start(s32[64]{0:T(128)} %param.12) | copy-start | bytes 772
  477.6 7.3 %copy-start.5 = (s32[128]{0:T(128)S(1)}, s32[128]{0:T(128)}, u32[]{:S(2)}) copy-start(s32[128]{0:T(128)} %param.13) | copy-start | bytes 1540
  558.4 22.0 %slice-start = ((bf16[128,36864]{1,0:T(8,128)(2,1)}), bf16[128,4096]{1,0:T(8,128)(2,1)S(1)}, s32[]{:S(2)}) async-start(bf16[128,36864]{1,0:T(8,128)(2,1)} %reshape.63), calls=%async_computation.5 | async-start | bytes 2097152 | tf_op jit(solution)/shard_map/split | solution.py:22
  565.6 24.5 %all-to-all-start.1 = ((f32[8,4,128,32]{2,3,1,0:T(8,128)}), f32[8,4,128,32]{2,3,1,0:T(8,128)}, u32[]{:S(2)}, u32[]{:S(2)}) async-start(f32[8,4,128,32]{2,3,1,0:T(8,128)} %broadcast_in_dim.41), calls=%async_computation.2 | async-start | bytes 1048576 | tf_op jit(solution)/shard_map/all_to_all | solution.py:28
Sparse Core Ops, SparseCore 0:
  60.1 465.5 all-gather.2
Sparse Core Ops, SparseCore 1:
  484.5 36.7 reduce-scatter.1
